TPU v7x, 32 devices: a whole 2x2x4 slice. The times are simulated.
32 devices in a mesh: gx: 4 (over z), gy: 2 (over y), gz: 4 (over x, core).
Axes of the slice: x: 2, y: 2, z: 4, core: 2. Of those that a mesh axis runs over, the one named last changes fastest.
Arguments:
- start_disp: float32 [3, 32, 16, 512], P(None, 'gx', 'gy', 'gz'), may hold values from -2 to 2
- inertial: float32 [3, 32, 16, 512], P(None, 'gx', 'gy', 'gz'), may hold values from -1 to 1
- material: int32 [32, 16, 512], P('gx', 'gy', 'gz'), may hold values from 0 to 7
- pinned: int32 [32, 16, 512], P('gx', 'gy', 'gz'), may hold values 0 or 1
- stiffness: float32 [8], replicated, may hold values from 3 to 100
Outputs:
- displacement: float32 [3, 32, 16, 512], P(None, 'gx', 'gy', 'gz')
All inputs are finite; a program needn't handle non-finite values. No bound on the sum of `pinned` on one device may be relied on, other than what follows from the above.
Results may differ from a plain program's by a relative error of at most 0.0003.
Values sent between devices are 32-bit elements; how exact they have to be, the bound alone decides.
A program may use at most 64 MiB of HBM per device.

v0:
```python
import jax
import jax.numpy as jnp
from jax import lax
from jax.sharding import PartitionSpec as P

ITERS = 4
POLAR_STEPS = 6
MATS = 8


inertia = 1.0
relax = 0.6
radius = 0.9


def with_halo(cells, sides, width):
    for axis, dim in sides:
        count = lax.axis_size(axis)
        ends = count - 1
        head = lax.slice_in_dim(cells, 0, width, axis=dim)
        tail = lax.slice_in_dim(cells, cells.shape[dim] - width, cells.shape[dim], axis=dim)
        cells = jnp.concatenate(
            [
                lax.ppermute(tail, axis, [(i, (i + 1) % count) for i in range(ends)]),
                cells,
                lax.ppermute(head, axis, [((i + 1) % count, i) for i in range(ends)]),
            ],
            axis=dim,
        )
    return cells


def forward_diff(field, axis):
    size = field.shape[axis]
    return lax.slice_in_dim(field, 1, size, axis=axis) - lax.slice_in_dim(
        field, 0, size - 1, axis=axis
    )


def pair_sum(field, axis):
    size = field.shape[axis]
    return lax.slice_in_dim(field, 1, size, axis=axis) + lax.slice_in_dim(
        field, 0, size - 1, axis=axis
    )


def gradient(field, axis):
    result = forward_diff(field, axis)
    for other in range(3):
        if other != axis:
            result = pair_sum(result, other)
    return 0.25 * result


def project(nodes, welem):
    deform = [
        [gradient(nodes[c], d) + (1.0 if c == d else 0.0) for d in range(3)] for c in range(3)
    ]
    total = sum((deform[c][d] * deform[c][d] for c in range(3) for d in range(3)))
    scale = jnp.maximum(jnp.sqrt(total / 3.0), 1.0)
    rotate = [[deform[c][d] / scale for d in range(3)] for c in range(3)]
    for step in range(POLAR_STEPS):
        middle = [
            [
                (1.5 if i == j else 0.0)
                - 0.5 * sum((rotate[k][i] * rotate[k][j] for k in range(3)))
                for j in range(3)
            ]
            for i in range(3)
        ]
        rotate = [
            [sum((rotate[c][j] * middle[j][d] for j in range(3))) for d in range(3)]
            for c in range(3)
        ]
    return [welem * (deform[c][d] - rotate[c][d]) for c in range(3) for d in range(3)]


def assemble(stress):
    forces = []
    for c in range(3):
        total = 0.0
        for d in range(3):
            term = stress[3 * c + d]
            for other in range(3):
                if other != d:
                    term = pair_sum(term, other)
            total = total - 0.25 * forward_diff(term, d)
        forces.append(total)
    return jnp.stack(forces)


def diagonal(welem):
    total = welem
    for axis in range(3):
        total = pair_sum(total, axis)
    return inertia + 3.0 / 16.0 * total


def node_halo(disp, weights):
    joined = jnp.concatenate([disp, weights[None]], axis=0)
    return with_halo(joined, (("gx", 1), ("gy", 2), ("gz", 3)), 1)


def per_device(start_disp, inertial, material, pinned, stiffness):
    size_x, size_y, size_z = material.shape
    grid_x = lax.broadcasted_iota(jnp.int32, material.shape, 0) + lax.axis_index("gx") * size_x
    grid_y = lax.broadcasted_iota(jnp.int32, material.shape, 1) + lax.axis_index("gy") * size_y
    grid_z = lax.broadcasted_iota(jnp.int32, material.shape, 2) + lax.axis_index("gz") * size_z
    valid = (
        (grid_x < size_x * lax.axis_size("gx") - 1)
        & (grid_y < size_y * lax.axis_size("gy") - 1)
        & (grid_z < size_z * lax.axis_size("gz") - 1)
    )
    table = jnp.zeros(material.shape, jnp.float32)
    for index in range(MATS):
        table = table + jnp.where(material == index, stiffness[index], 0.0)
    weights = jnp.where(valid, table, 0.0)
    pins = pinned[None] > 0
    disp = jnp.where(pins, inertial, start_disp)
    previous = disp
    omega = 1.0
    for step in range(ITERS):
        padded = node_halo(disp, weights)
        welem = padded[3, : size_x + 1, : size_y + 1, : size_z + 1]
        diag = diagonal(welem)
        forces = assemble(project([padded[0], padded[1], padded[2]], welem))
        target = disp - relax * (inertia * (disp - inertial) + forces) / diag[None]
        if step == 0:
            fresh = target
        else:
            omega = (
                2.0 / (2.0 - radius * radius)
                if step == 1
                else 4.0 / (4.0 - radius * radius * omega)
            )
            fresh = omega * (target - previous) + previous
        fresh = jnp.where(pins, inertial, fresh)
        previous = disp
        disp = fresh
    return disp


def solution(mesh):
    placed = (
        P(None, "gx", "gy", "gz"),
        P(None, "gx", "gy", "gz"),
        P("gx", "gy", "gz"),
        P("gx", "gy", "gz"),
        P(),
    )
    return jax.shard_map(
        per_device, mesh=mesh, in_specs=placed, out_specs=P(None, "gx", "gy", "gz"), check_vma=False
    )
```

profile of v0, /device:TPU:1, one launch (start us, length us, event | category | flops | bytes accessed | tf_op | source)
XLA Modules:
  0.0 147.5 jit_solution(12972849443909755106)
XLA Ops:
  3.4 4.9 %select_bitcast_fusion = f32[1,8,8,128]{3,2,1,0:T(8,128)S(1)} fusion(s32[8,8,128]{2,1,0:T(8,128)S(1)} %copy-done.3, f32[]{:T(128)} %bitcast.7, f32[]{:T(128)} %bitcast.6, f32[]{:T(128)} %bitcast.5, f32[]{:T(128)} %bitcast.4, f32[]{:T(128)} %bitcast.3, f32[]{:T(128)} %bitcast.2, f32[]{:T(128)} %bitcast.1, f32[]{:T(128)} %bitcast, ...), kind=kLoop, calls=%fused_computation.883 | loop fusion | flops 212992 | bytes 65712 | tf_op jit(solution)/shard_map/broadcast_in_dim | solution.py:100
  8.3 4.0 %collective-permute-start = (f32[4,1,8,128]{3,2,1,0:T(8,128)S(1)}, f32[4,1,8,128]{3,2,1,0:T(8,128)S(1)}, u32[]{:S(2)}, u32[]{:S(2)}) collective-permute-start(f32[4,1,8,128]{3,2,1,0:T(8,128)S(1)} %get-tuple-element.373), channel_id=1, source_target_pairs={{0,8},{8,16},{16,24},{1,9},{9,17},{17,25},{2,10},{10,18},{18,26},{... | collective-permute-start | bytes 49160 | tf_op jit(solution)/shard_map/ppermute | solution.py:24
  13.6 3.2 %collective-permute-done.1 = f32[4,1,8,128]{3,2,1,0:T(8,128)S(1)} collective-permute-done((f32[4,1,8,128]{3,2,1,0:T(8,128)S(1)}, f32[4,1,8,128]{3,2,1,0:T(8,128)S(1)}, u32[]{:S(2)}, u32[]{:S(2)}) %collective-permute-start.1) | collective-permute-done | bytes 16416 | tf_op jit(solution)/shard_map/ppermute | solution.py:26
  16.9 3.1 %collective-permute-start.2 = (f32[4,10,1,128]{3,2,1,0:T(1,128)S(1)}, f32[4,10,1,128]{3,2,1,0:T(1,128)S(1)}, u32[]{:S(2)}, u32[]{:S(2)}) collective-permute-start(f32[4,10,1,128]{3,2,1,0:T(1,128)S(1)} %get-tuple-element.365), channel_id=1, source_target_pairs={{0,4},{1,5},{2,6},{3,7},{8,12},{9,13},{10,14},{11,15},{16,20},{17,... | collective-permute-start | bytes 61448 | tf_op jit(solution)/shard_map/ppermute | solution.py:24
  21.3 3.2 %collective-permute-done.3 = f32[4,10,1,128]{3,2,1,0:T(1,128)S(1)} collective-permute-done((f32[4,10,1,128]{3,2,1,0:T(1,128)S(1)}, f32[4,10,1,128]{3,2,1,0:T(1,128)S(1)}, u32[]{:S(2)}, u32[]{:S(2)}) %collective-permute-start.3) | collective-permute-done | bytes 20512 | tf_op jit(solution)/shard_map/ppermute | solution.py:26
  24.8 6.5 %collective-permute-start.4 = (f32[4,10,10,1]{3,2,1,0:T(8,128)S(1)}, f32[4,10,10,1]{3,2,1,0:T(8,128)S(1)}, u32[]{:S(2)}, u32[]{:S(2)}) collective-permute-start(f32[4,10,10,1]{3,2,1,0:T(8,128)S(1)} %get-tuple-element.358), channel_id=1, source_target_pairs={{0,1},{1,2},{2,3},{4,5},{5,6},{6,7},{8,9},{9,10},{10,11},{12,13},{... | collective-permute-start | bytes 4808 | tf_op jit(solution)/shard_map/ppermute | solution.py:24
  35.3 4.4 %collective-permute-done.5 = f32[4,10,10,1]{3,2,1,0:T(8,128)S(1)} collective-permute-done((f32[4,10,10,1]{3,2,1,0:T(8,128)S(1)}, f32[4,10,10,1]{3,2,1,0:T(8,128)S(1)}, u32[]{:S(2)}, u32[]{:S(2)}) %collective-permute-start.5) | collective-permute-done | bytes 1632 | tf_op jit(solution)/shard_map/ppermute | solution.py:26
  47.4 3.2 %collective-permute-start.6 = (f32[4,1,8,128]{3,2,1,0:T(8,128)S(1)}, f32[4,1,8,128]{3,2,1,0:T(8,128)S(1)}, u32[]{:S(2)}, u32[]{:S(2)}) collective-permute-start(f32[4,1,8,128]{3,2,1,0:T(8,128)S(1)} %get-tuple-element.371), channel_id=1, source_target_pairs={{0,8},{8,16},{16,24},{1,9},{9,17},{17,25},{2,10},{10,18},{18,26},{... | collective-permute-start | bytes 49160 | tf_op jit(solution)/shard_map/ppermute | solution.py:24
  51.9 3.2 %collective-permute-done.7 = f32[4,1,8,128]{3,2,1,0:T(8,128)S(1)} collective-permute-done((f32[4,1,8,128]{3,2,1,0:T(8,128)S(1)}, f32[4,1,8,128]{3,2,1,0:T(8,128)S(1)}, u32[]{:S(2)}, u32[]{:S(2)}) %collective-permute-start.7) | collective-permute-done | bytes 16416 | tf_op jit(solution)/shard_map/ppermute | solution.py:26
  57.8 3.2 %collective-permute-done.9 = f32[4,10,1,128]{3,2,1,0:T(1,128)S(1)} collective-permute-done((f32[4,10,1,128]{3,2,1,0:T(1,128)S(1)}, f32[4,10,1,128]{3,2,1,0:T(1,128)S(1)}, u32[]{:S(2)}, u32[]{:S(2)}) %collective-permute-start.9) | collective-permute-done | bytes 20512 | tf_op jit(solution)/shard_map/ppermute | solution.py:26
  61.2 4.6 %collective-permute-start.10 = (f32[4,10,10,1]{3,2,1,0:T(8,128)S(1)}, f32[4,10,10,1]{3,2,1,0:T(8,128)S(1)}, u32[]{:S(2)}, u32[]{:S(2)}) collective-permute-start(f32[4,10,10,1]{3,2,1,0:T(8,128)S(1)} %get-tuple-element.356), channel_id=1, source_target_pairs={{0,1},{1,2},{2,3},{4,5},{5,6},{6,7},{8,9},{9,10},{10,11},{12,13},{... | collective-permute-start | bytes 4808 | tf_op jit(solution)/shard_map/ppermute | solution.py:24
  65.8 2.1 %collective-permute-start.11 = (f32[4,10,10,1]{3,2,1,0:T(8,128)S(1)}, f32[4,10,10,1]{3,2,1,0:T(8,128)S(1)}, u32[]{:S(2)}, u32[]{:S(2)}) collective-permute-start(f32[4,10,10,1]{3,2,1,0:T(8,128)S(1)} %get-tuple-element.355), channel_id=1, source_target_pairs={{1,0},{2,1},{3,2},{5,4},{6,5},{7,6},{9,8},{10,9},{11,10},{13,12},{... | collective-permute-start | bytes 4808 | tf_op jit(solution)/shard_map/ppermute | solution.py:26
  69.8 4.4 %collective-permute-done.11 = f32[4,10,10,1]{3,2,1,0:T(8,128)S(1)} collective-permute-done((f32[4,10,10,1]{3,2,1,0:T(8,128)S(1)}, f32[4,10,10,1]{3,2,1,0:T(8,128)S(1)}, u32[]{:S(2)}, u32[]{:S(2)}) %collective-permute-start.11) | collective-permute-done | bytes 1632 | tf_op jit(solution)/shard_map/ppermute | solution.py:26
  81.1 3.2 %collective-permute-start.12 = (f32[4,1,8,128]{3,2,1,0:T(8,128)S(1)}, f32[4,1,8,128]{3,2,1,0:T(8,128)S(1)}, u32[]{:S(2)}, u32[]{:S(2)}) collective-permute-start(f32[4,1,8,128]{3,2,1,0:T(8,128)S(1)} %get-tuple-element.369), channel_id=1, source_target_pairs={{0,8},{8,16},{16,24},{1,9},{9,17},{17,25},{2,10},{10,18},{18,26},{... | collective-permute-start | bytes 49160 | tf_op jit(solution)/shard_map/ppermute | solution.py:24
  85.6 3.2 %collective-permute-done.13 = f32[4,1,8,128]{3,2,1,0:T(8,128)S(1)} collective-permute-done((f32[4,1,8,128]{3,2,1,0:T(8,128)S(1)}, f32[4,1,8,128]{3,2,1,0:T(8,128)S(1)}, u32[]{:S(2)}, u32[]{:S(2)}) %collective-permute-start.13) | collective-permute-done | bytes 16416 | tf_op jit(solution)/shard_map/ppermute | solution.py:26
  91.5 3.2 %collective-permute-done.15 = f32[4,10,1,128]{3,2,1,0:T(1,128)S(1)} collective-permute-done((f32[4,10,1,128]{3,2,1,0:T(1,128)S(1)}, f32[4,10,1,128]{3,2,1,0:T(1,128)S(1)}, u32[]{:S(2)}, u32[]{:S(2)}) %collective-permute-start.15) | collective-permute-done | bytes 20512 | tf_op jit(solution)/shard_map/ppermute | solution.py:26
  94.9 4.6 %collective-permute-start.16 = (f32[4,10,10,1]{3,2,1,0:T(8,128)S(1)}, f32[4,10,10,1]{3,2,1,0:T(8,128)S(1)}, u32[]{:S(2)}, u32[]{:S(2)}) collective-permute-start(f32[4,10,10,1]{3,2,1,0:T(8,128)S(1)} %get-tuple-element.354), channel_id=1, source_target_pairs={{0,1},{1,2},{2,3},{4,5},{5,6},{6,7},{8,9},{9,10},{10,11},{12,13},{... | collective-permute-start | bytes 4808 | tf_op jit(solution)/shard_map/ppermute | solution.py:24
  99.5 2.1 %collective-permute-start.17 = (f32[4,10,10,1]{3,2,1,0:T(8,128)S(1)}, f32[4,10,10,1]{3,2,1,0:T(8,128)S(1)}, u32[]{:S(2)}, u32[]{:S(2)}) collective-permute-start(f32[4,10,10,1]{3,2,1,0:T(8,128)S(1)} %get-tuple-element.353), channel_id=1, source_target_pairs={{1,0},{2,1},{3,2},{5,4},{6,5},{7,6},{9,8},{10,9},{11,10},{13,12},{... | collective-permute-start | bytes 4808 | tf_op jit(solution)/shard_map/ppermute | solution.py:26
  103.5 4.4 %collective-permute-done.17 = f32[4,10,10,1]{3,2,1,0:T(8,128)S(1)} collective-permute-done((f32[4,10,10,1]{3,2,1,0:T(8,128)S(1)}, f32[4,10,10,1]{3,2,1,0:T(8,128)S(1)}, u32[]{:S(2)}, u32[]{:S(2)}) %collective-permute-start.17) | collective-permute-done | bytes 1632 | tf_op jit(solution)/shard_map/ppermute | solution.py:26
  117.7 3.2 %collective-permute-done.19 = f32[4,1,8,128]{3,2,1,0:T(8,128)S(1)} collective-permute-done((f32[4,1,8,128]{3,2,1,0:T(8,128)S(1)}, f32[4,1,8,128]{3,2,1,0:T(8,128)S(1)}, u32[]{:S(2)}, u32[]{:S(2)}) %collective-permute-start.19) | collective-permute-done | bytes 16416 | tf_op jit(solution)/shard_map/ppermute | solution.py:26
  123.6 3.2 %collective-permute-done.21 = f32[4,10,1,128]{3,2,1,0:T(1,128)S(1)} collective-permute-done((f32[4,10,1,128]{3,2,1,0:T(1,128)S(1)}, f32[4,10,1,128]{3,2,1,0:T(1,128)S(1)}, u32[]{:S(2)}, u32[]{:S(2)}) %collective-permute-start.21) | collective-permute-done | bytes 20512 | tf_op jit(solution)/shard_map/ppermute | solution.py:26
  127.0 4.6 %collective-permute-start.22 = (f32[4,10,10,1]{3,2,1,0:T(8,128)S(1)}, f32[4,10,10,1]{3,2,1,0:T(8,128)S(1)}, u32[]{:S(2)}, u32[]{:S(2)}) collective-permute-start(f32[4,10,10,1]{3,2,1,0:T(8,128)S(1)} %get-tuple-element.352), channel_id=1, source_target_pairs={{0,1},{1,2},{2,3},{4,5},{5,6},{6,7},{8,9},{9,10},{10,11},{12,13},{... | collective-permute-start | bytes 4808 | tf_op jit(solution)/shard_map/ppermute | solution.py:24
  131.7 2.2 %collective-permute-start.23 = (f32[4,10,10,1]{3,2,1,0:T(8,128)S(1)}, f32[4,10,10,1]{3,2,1,0:T(8,128)S(1)}, u32[]{:S(2)}, u32[]{:S(2)}) collective-permute-start(f32[4,10,10,1]{3,2,1,0:T(8,128)S(1)} %get-tuple-element.351), channel_id=1, source_target_pairs={{1,0},{2,1},{3,2},{5,4},{6,5},{7,6},{9,8},{10,9},{11,10},{13,12},{... | collective-permute-start | bytes 4808 | tf_op jit(solution)/shard_map/ppermute | solution.py:26
  135.7 4.4 %collective-permute-done.23 = f32[4,10,10,1]{3,2,1,0:T(8,128)S(1)} collective-permute-done((f32[4,10,10,1]{3,2,1,0:T(8,128)S(1)}, f32[4,10,10,1]{3,2,1,0:T(8,128)S(1)}, u32[]{:S(2)}, u32[]{:S(2)}) %collective-permute-start.23) | collective-permute-done | bytes 1632 | tf_op jit(solution)/shard_map/ppermute | solution.py:26
  (282 shorter events, 57.3 us)
Async XLA Ops:
  8.3 5.3 %collective-permute-start = (f32[4,1,8,128]{3,2,1,0:T(8,128)S(1)}, f32[4,1,8,128]{3,2,1,0:T(8,128)S(1)}, u32[]{:S(2)}, u32[]{:S(2)}) collective-permute-start(f32[4,1,8,128]{3,2,1,0:T(8,128)S(1)} %get-tuple-element.373), channel_id=1, source_target_pairs={{0,8},{8,16},{16,24},{1,9},{9,17},{17,25},{2,10},{10,18},{18,26},{... | collective-permute-start | bytes 49160 | tf_op jit(solution)/shard_map/ppermute | solution.py:24
  12.3 4.5 %collective-permute-start.1 = (f32[4,1,8,128]{3,2,1,0:T(8,128)S(1)}, f32[4,1,8,128]{3,2,1,0:T(8,128)S(1)}, u32[]{:S(2)}, u32[]{:S(2)}) collective-permute-start(f32[4,1,8,128]{3,2,1,0:T(8,128)S(1)} %get-tuple-element.301), channel_id=1, source_target_pairs={{8,0},{16,8},{24,16},{9,1},{17,9},{25,17},{10,2},{18,10},{26,18},{... | collective-permute-start | bytes 49160 | tf_op jit(solution)/shard_map/ppermute | solution.py:26
  16.9 4.5 %collective-permute-start.2 = (f32[4,10,1,128]{3,2,1,0:T(1,128)S(1)}, f32[4,10,1,128]{3,2,1,0:T(1,128)S(1)}, u32[]{:S(2)}, u32[]{:S(2)}) collective-permute-start(f32[4,10,1,128]{3,2,1,0:T(1,128)S(1)} %get-tuple-element.365), channel_id=1, source_target_pairs={{0,4},{1,5},{2,6},{3,7},{8,12},{9,13},{10,14},{11,15},{16,20},{17,... | collective-permute-start | bytes 61448 | tf_op jit(solution)/shard_map/ppermute | solution.py:24
  20.0 4.5 %collective-permute-start.3 = (f32[4,10,1,128]{3,2,1,0:T(1,128)S(1)}, f32[4,10,1,128]{3,2,1,0:T(1,128)S(1)}, u32[]{:S(2)}, u32[]{:S(2)}) collective-permute-start(f32[4,10,1,128]{3,2,1,0:T(1,128)S(1)} %get-tuple-element.366), channel_id=1, source_target_pairs={{4,0},{5,1},{6,2},{7,3},{12,8},{13,9},{14,10},{15,11},{20,16},{21,... | collective-permute-start | bytes 61448 | tf_op jit(solution)/shard_map/ppermute | solution.py:26
  24.8 10.5 %collective-permute-start.4 = (f32[4,10,10,1]{3,2,1,0:T(8,128)S(1)}, f32[4,10,10,1]{3,2,1,0:T(8,128)S(1)}, u32[]{:S(2)}, u32[]{:S(2)}) collective-permute-start(f32[4,10,10,1]{3,2,1,0:T(8,128)S(1)} %get-tuple-element.358), channel_id=1, source_target_pairs={{0,1},{1,2},{2,3},{4,5},{5,6},{6,7},{8,9},{9,10},{10,11},{12,13},{... | collective-permute-start | bytes 4808 | tf_op jit(solution)/shard_map/ppermute | solution.py:24
  31.3 8.4 %collective-permute-start.5 = (f32[4,10,10,1]{3,2,1,0:T(8,128)S(1)}, f32[4,10,10,1]{3,2,1,0:T(8,128)S(1)}, u32[]{:S(2)}, u32[]{:S(2)}) collective-permute-start(f32[4,10,10,1]{3,2,1,0:T(8,128)S(1)} %get-tuple-element.357), channel_id=1, source_target_pairs={{1,0},{2,1},{3,2},{5,4},{6,5},{7,6},{9,8},{10,9},{11,10},{13,12},{... | collective-permute-start | bytes 4808 | tf_op jit(solution)/shard_map/ppermute | solution.py:26
  47.4 4.5 %collective-permute-start.6 = (f32[4,1,8,128]{3,2,1,0:T(8,128)S(1)}, f32[4,1,8,128]{3,2,1,0:T(8,128)S(1)}, u32[]{:S(2)}, u32[]{:S(2)}) collective-permute-start(f32[4,1,8,128]{3,2,1,0:T(8,128)S(1)} %get-tuple-element.371), channel_id=1, source_target_pairs={{0,8},{8,16},{16,24},{1,9},{9,17},{17,25},{2,10},{10,18},{18,26},{... | collective-permute-start | bytes 49160 | tf_op jit(solution)/shard_map/ppermute | solution.py:24
  50.6 4.5 %collective-permute-start.7 = (f32[4,1,8,128]{3,2,1,0:T(8,128)S(1)}, f32[4,1,8,128]{3,2,1,0:T(8,128)S(1)}, u32[]{:S(2)}, u32[]{:S(2)}) collective-permute-start(f32[4,1,8,128]{3,2,1,0:T(8,128)S(1)} %get-tuple-element.372), channel_id=1, source_target_pairs={{8,0},{16,8},{24,16},{9,1},{17,9},{25,17},{10,2},{18,10},{26,18},{... | collective-permute-start | bytes 49160 | tf_op jit(solution)/shard_map/ppermute | solution.py:26
  55.1 2.7 %collective-permute-start.8 = (f32[4,10,1,128]{3,2,1,0:T(1,128)S(1)}, f32[4,10,1,128]{3,2,1,0:T(1,128)S(1)}, u32[]{:S(2)}, u32[]{:S(2)}) collective-permute-start(f32[4,10,1,128]{3,2,1,0:T(1,128)S(1)} %get-tuple-element.363), channel_id=1, source_target_pairs={{0,4},{1,5},{2,6},{3,7},{8,12},{9,13},{10,14},{11,15},{16,20},{17,... | collective-permute-start | bytes 61448 | tf_op jit(solution)/shard_map/ppermute | solution.py:24
  56.5 4.5 %collective-permute-start.9 = (f32[4,10,1,128]{3,2,1,0:T(1,128)S(1)}, f32[4,10,1,128]{3,2,1,0:T(1,128)S(1)}, u32[]{:S(2)}, u32[]{:S(2)}) collective-permute-start(f32[4,10,1,128]{3,2,1,0:T(1,128)S(1)} %get-tuple-element.364), channel_id=1, source_target_pairs={{4,0},{5,1},{6,2},{7,3},{12,8},{13,9},{14,10},{15,11},{20,16},{21,... | collective-permute-start | bytes 61448 | tf_op jit(solution)/shard_map/ppermute | solution.py:26
  61.2 8.6 %collective-permute-start.10 = (f32[4,10,10,1]{3,2,1,0:T(8,128)S(1)}, f32[4,10,10,1]{3,2,1,0:T(8,128)S(1)}, u32[]{:S(2)}, u32[]{:S(2)}) collective-permute-start(f32[4,10,10,1]{3,2,1,0:T(8,128)S(1)} %get-tuple-element.356), channel_id=1, source_target_pairs={{0,1},{1,2},{2,3},{4,5},{5,6},{6,7},{8,9},{9,10},{10,11},{12,13},{... | collective-permute-start | bytes 4808 | tf_op jit(solution)/shard_map/ppermute | solution.py:24
  65.8 8.4 %collective-permute-start.11 = (f32[4,10,10,1]{3,2,1,0:T(8,128)S(1)}, f32[4,10,10,1]{3,2,1,0:T(8,128)S(1)}, u32[]{:S(2)}, u32[]{:S(2)}) collective-permute-start(f32[4,10,10,1]{3,2,1,0:T(8,128)S(1)} %get-tuple-element.355), channel_id=1, source_target_pairs={{1,0},{2,1},{3,2},{5,4},{6,5},{7,6},{9,8},{10,9},{11,10},{13,12},{... | collective-permute-start | bytes 4808 | tf_op jit(solution)/shard_map/ppermute | solution.py:26
  81.1 4.5 %collective-permute-start.12 = (f32[4,1,8,128]{3,2,1,0:T(8,128)S(1)}, f32[4,1,8,128]{3,2,1,0:T(8,128)S(1)}, u32[]{:S(2)}, u32[]{:S(2)}) collective-permute-start(f32[4,1,8,128]{3,2,1,0:T(8,128)S(1)} %get-tuple-element.369), channel_id=1, source_target_pairs={{0,8},{8,16},{16,24},{1,9},{9,17},{17,25},{2,10},{10,18},{18,26},{... | collective-permute-start | bytes 49160 | tf_op jit(solution)/shard_map/ppermute | solution.py:24
  84.3 4.5 %collective-permute-start.13 = (f32[4,1,8,128]{3,2,1,0:T(8,128)S(1)}, f32[4,1,8,128]{3,2,1,0:T(8,128)S(1)}, u32[]{:S(2)}, u32[]{:S(2)}) collective-permute-start(f32[4,1,8,128]{3,2,1,0:T(8,128)S(1)} %get-tuple-element.370), channel_id=1, source_target_pairs={{8,0},{16,8},{24,16},{9,1},{17,9},{25,17},{10,2},{18,10},{26,18},{... | collective-permute-start | bytes 49160 | tf_op jit(solution)/shard_map/ppermute | solution.py:26
  88.8 2.7 %collective-permute-start.14 = (f32[4,10,1,128]{3,2,1,0:T(1,128)S(1)}, f32[4,10,1,128]{3,2,1,0:T(1,128)S(1)}, u32[]{:S(2)}, u32[]{:S(2)}) collective-permute-start(f32[4,10,1,128]{3,2,1,0:T(1,128)S(1)} %get-tuple-element.361), channel_id=1, source_target_pairs={{0,4},{1,5},{2,6},{3,7},{8,12},{9,13},{10,14},{11,15},{16,20},{17,... | collective-permute-start | bytes 61448 | tf_op jit(solution)/shard_map/ppermute | solution.py:24
  90.2 4.5 %collective-permute-start.15 = (f32[4,10,1,128]{3,2,1,0:T(1,128)S(1)}, f32[4,10,1,128]{3,2,1,0:T(1,128)S(1)}, u32[]{:S(2)}, u32[]{:S(2)}) collective-permute-start(f32[4,10,1,128]{3,2,1,0:T(1,128)S(1)} %get-tuple-element.362), channel_id=1, source_target_pairs={{4,0},{5,1},{6,2},{7,3},{12,8},{13,9},{14,10},{15,11},{20,16},{21,... | collective-permute-start | bytes 61448 | tf_op jit(solution)/shard_map/ppermute | solution.py:26
  94.9 8.6 %collective-permute-start.16 = (f32[4,10,10,1]{3,2,1,0:T(8,128)S(1)}, f32[4,10,10,1]{3,2,1,0:T(8,128)S(1)}, u32[]{:S(2)}, u32[]{:S(2)}) collective-permute-start(f32[4,10,10,1]{3,2,1,0:T(8,128)S(1)} %get-tuple-element.354), channel_id=1, source_target_pairs={{0,1},{1,2},{2,3},{4,5},{5,6},{6,7},{8,9},{9,10},{10,11},{12,13},{... | collective-permute-start | bytes 4808 | tf_op jit(solution)/shard_map/ppermute | solution.py:24
  99.5 8.4 %collective-permute-start.17 = (f32[4,10,10,1]{3,2,1,0:T(8,128)S(1)}, f32[4,10,10,1]{3,2,1,0:T(8,128)S(1)}, u32[]{:S(2)}, u32[]{:S(2)}) collective-permute-start(f32[4,10,10,1]{3,2,1,0:T(8,128)S(1)} %get-tuple-element.353), channel_id=1, source_target_pairs={{1,0},{2,1},{3,2},{5,4},{6,5},{7,6},{9,8},{10,9},{11,10},{13,12},{... | collective-permute-start | bytes 4808 | tf_op jit(solution)/shard_map/ppermute | solution.py:26
  114.8 3.0 %collective-permute-start.18 = (f32[4,1,8,128]{3,2,1,0:T(8,128)S(1)}, f32[4,1,8,128]{3,2,1,0:T(8,128)S(1)}, u32[]{:S(2)}, u32[]{:S(2)}) collective-permute-start(f32[4,1,8,128]{3,2,1,0:T(8,128)S(1)} %get-tuple-element.367), channel_id=1, source_target_pairs={{0,8},{8,16},{16,24},{1,9},{9,17},{17,25},{2,10},{10,18},{18,26},{... | collective-permute-start | bytes 49160 | tf_op jit(solution)/shard_map/ppermute | solution.py:24
  116.4 4.5 %collective-permute-start.19 = (f32[4,1,8,128]{3,2,1,0:T(8,128)S(1)}, f32[4,1,8,128]{3,2,1,0:T(8,128)S(1)}, u32[]{:S(2)}, u32[]{:S(2)}) collective-permute-start(f32[4,1,8,128]{3,2,1,0:T(8,128)S(1)} %get-tuple-element.368), channel_id=1, source_target_pairs={{8,0},{16,8},{24,16},{9,1},{17,9},{25,17},{10,2},{18,10},{26,18},{... | collective-permute-start | bytes 49160 | tf_op jit(solution)/shard_map/ppermute | solution.py:26
  120.9 2.7 %collective-permute-start.20 = (f32[4,10,1,128]{3,2,1,0:T(1,128)S(1)}, f32[4,10,1,128]{3,2,1,0:T(1,128)S(1)}, u32[]{:S(2)}, u32[]{:S(2)}) collective-permute-start(f32[4,10,1,128]{3,2,1,0:T(1,128)S(1)} %get-tuple-element.359), channel_id=1, source_target_pairs={{0,4},{1,5},{2,6},{3,7},{8,12},{9,13},{10,14},{11,15},{16,20},{17,... | collective-permute-start | bytes 61448 | tf_op jit(solution)/shard_map/ppermute | solution.py:24
  122.3 4.5 %collective-permute-start.21 = (f32[4,10,1,128]{3,2,1,0:T(1,128)S(1)}, f32[4,10,1,128]{3,2,1,0:T(1,128)S(1)}, u32[]{:S(2)}, u32[]{:S(2)}) collective-permute-start(f32[4,10,1,128]{3,2,1,0:T(1,128)S(1)} %get-tuple-element.360), channel_id=1, source_target_pairs={{4,0},{5,1},{6,2},{7,3},{12,8},{13,9},{14,10},{15,11},{20,16},{21,... | collective-permute-start | bytes 61448 | tf_op jit(solution)/shard_map/ppermute | solution.py:26
  127.0 8.6 %collective-permute-start.22 = (f32[4,10,10,1]{3,2,1,0:T(8,128)S(1)}, f32[4,10,10,1]{3,2,1,0:T(8,128)S(1)}, u32[]{:S(2)}, u32[]{:S(2)}) collective-permute-start(f32[4,10,10,1]{3,2,1,0:T(8,128)S(1)} %get-tuple-element.352), channel_id=1, source_target_pairs={{0,1},{1,2},{2,3},{4,5},{5,6},{6,7},{8,9},{9,10},{10,11},{12,13},{... | collective-permute-start | bytes 4808 | tf_op jit(solution)/shard_map/ppermute | solution.py:24
  131.7 8.4 %collective-permute-start.23 = (f32[4,10,10,1]{3,2,1,0:T(8,128)S(1)}, f32[4,10,10,1]{3,2,1,0:T(8,128)S(1)}, u32[]{:S(2)}, u32[]{:S(2)}) collective-permute-start(f32[4,10,10,1]{3,2,1,0:T(8,128)S(1)} %get-tuple-element.351), channel_id=1, source_target_pairs={{1,0},{2,1},{3,2},{5,4},{6,5},{7,6},{9,8},{10,9},{11,10},{13,12},{... | collective-permute-start | bytes 4808 | tf_op jit(solution)/shard_map/ppermute | solution.py:26
  (4 other events, 4.2 us)
where the time goes:
time: 148 us; the launch traced here: 147 us
  starting transfers between devices  58.3 us (39%)
  waiting for transfers between devices  50.8 us (34%)
  other arithmetic  32.5 us (22%)
  local copies, waits for them, and re-layouts  4.11 us (3%)
  between operations  1.78 us (1%)
    ppermute x12, waiting for transfers between devices, with_halo(): lax.ppermute(head, axis, [((i + 1) % count, i) for i in range(ends)])  43.1 us
    ppermute x12, starting transfers between devices, with_halo(): lax.ppermute(tail, axis, [(i, (i + 1) % count) for i in range(ends)])  39.6 us
    ppermute x12, starting transfers between devices, with_halo(): lax.ppermute(head, axis, [((i + 1) % count, i) for i in range(ends)])  18.7 us
    sub x24, other arithmetic, project(): (1.5 if i == j else 0.0) - 0.5 * sum((rotate[k][i] * rotate[k][j] for k i...  10.1 us
    ppermute x12, waiting for transfers between devices, with_halo(): lax.ppermute(tail, axis, [(i, (i + 1) % count) for i in range(ends)])  7.64 us
    mul x24, other arithmetic, project(): welem * (deform[c][d] - rotate[c][d])  5.75 us
    broadcast_in_dim x1, other arithmetic, node_halo(): joined = jnp.concatenate([disp, weights[None]], axis=0)  4.89 us
    concatenate x16, other arithmetic, with_halo(): jnp.concatenate([lax.ppermute(tail, axis, [(i, (i + 1) % count) for i in...  3.9 us
  transfers between devices with their start and end apart: 24, of which 16 were waited for; matrix products, arithmetic and copies ran while one was open for 0% of the time, Pallas kernels for 0%

commit v1 on v0

v1 whole, which is shorter than its diff:
```python
import functools

import jax
import jax.numpy as jnp
from jax import lax
from jax.experimental import pallas as pl
from jax.experimental.pallas import tpu as pltpu
from jax.sharding import PartitionSpec as P

ITERS = 4
POLAR_STEPS = 6
MATS = 8

relax = 0.6
radius = 0.9
HALO = ITERS
SLOT = 2 * HALO
NARR = 8
AXES = ("gx", "gy", "gz")


def node_terms(u, uz, roll_y):
    zs, zd = uz + u, uz - u
    ys, yd = roll_y(zs), roll_y(zd)
    return zs + ys, ys - zs, zd + yd


def stretch(low, high):
    deform = []
    for c in range(3):
        dx = high[c][0] - low[c][0]
        dy = high[c][1] + low[c][1]
        dz = high[c][2] + low[c][2]
        row = [dx, dy, dz]
        row[c] = row[c] + 1.0
        deform.append(row)
    return deform


def stress(deform, w):
    total = None
    for c in range(3):
        for d in range(3):
            sq = deform[c][d] * deform[c][d]
            total = sq if total is None else total + sq
    inv = jnp.minimum(lax.rsqrt(total * (1.0 / 3.0)), 1.0) * (0.5**0.5)
    z = [[deform[c][d] * inv for d in range(3)] for c in range(3)]

    def polar(_, flat):
        z = [flat[3 * c : 3 * c + 3] for c in range(3)]
        s = {}
        for i in range(3):
            for j in range(i, 3):
                s[i, j] = z[0][i] * z[0][j] + z[1][i] * z[1][j] + z[2][i] * z[2][j]
        m = [1.5 - s[i, i] for i in range(3)]
        out = []
        for c in range(3):
            a, b, e = z[c]
            out.append(a * m[0] - b * s[0, 1] - e * s[0, 2])
            out.append(b * m[1] - a * s[0, 1] - e * s[1, 2])
            out.append(e * m[2] - a * s[0, 2] - b * s[1, 2])
        return tuple(out)

    flat = lax.fori_loop(
        0, POLAR_STEPS, polar, tuple(z[c][d] for c in range(3) for d in range(3)), unroll=True
    )
    return [w * (deform[k // 3][k % 3] - flat[k] * (2.0**0.5)) for k in range(9)]


def node_sums(before, here, roll_y):
    a = before[0] - here[0]
    b = before[1] + here[1]
    e = before[2] + here[2]
    g = (a - b) + roll_y(a + b)
    e = e + roll_y(e)
    return g - e, g + e


def advance(u, prev, inert, pin, rate, f, omega):
    target = u - rate * ((u - inert) + f)
    fresh = target if omega is None else omega * (target - prev) + prev
    return jnp.where(pin > 0.0, inert, fresh)


def kernel(
    counts, start, inertial, material, pinned, stiff, out,
    xe, sy, ry, ext, az, rz, prev, rate, terms, press, strip, sprev, srate, hz,
    send_sem, recv_sem,
):
    size_x, size_y, size_z = material.shape
    here = [lax.axis_index(a) for a in AXES]
    has = [[here[i] > 0, here[i] < counts[i] - 1] for i in range(3)]

    sub = lax.broadcasted_iota(jnp.int32, (size_y, size_z), 0)
    lane = lax.broadcasted_iota(jnp.int32, (size_y, size_z), 1)
    inside = ((sub < size_y - 1) | has[1][1]) & ((lane < size_z - 1) | has[2][1])
    quarter = [stiff[i] * 0.25 for i in range(MATS)]

    barrier = pltpu.get_barrier_semaphore()

    def peer(i, side):
        return {AXES[i]: here[i] + (1 if side else -1)}

    for i in range(3):
        for side in range(2):
            @pl.when(has[i][side])
            def _(i=i, side=side):
                pl.semaphore_signal(
                    barrier, inc=1, device_id=peer(i, side), device_id_type=pl.DeviceIdType.MESH
                )

    def pack_y(x, _):
        for p in range(NARR // 2):
            first, second = xe[2 * p, x], xe[2 * p + 1, x]
            low = jnp.where(sub < HALO, first, pltpu.roll(second, HALO, 0))
            high = jnp.where(sub < HALO, pltpu.roll(first, HALO, 0), second)
            sy[0, p, x] = low
            sy[1, p, x] = high
        return 0

    def own_plane(x, _):
        mat = material[x]
        w = jnp.zeros((size_y, size_z), jnp.float32)
        for index in range(MATS):
            w = jnp.where(mat == index, quarter[index], w)
        keep = inside & ((x < size_x - 1) | has[0][1])
        xe[6, x + HALO] = jnp.where(keep, w, 0.0)
        pins = pinned[x] > 0
        xe[7, x + HALO] = jnp.where(pins, 1.0, 0.0)
        for c in range(3):
            inert = inertial[c, x]
            xe[3 + c, x + HALO] = inert
            xe[c, x + HALO] = jnp.where(pins, inert, start[c, x])
        pack_y(x + HALO, 0)
        return 0

    lax.fori_loop(0, size_x, own_plane, 0)

    def zero(ref, lo, n):
        def body(x, _):
            for a in range(ref.shape[0]):
                ref[a, x] = jnp.zeros(ref.shape[2:], jnp.float32)
            return 0
        lax.fori_loop(lo, lo + n, body, 0)

    top = HALO + size_x
    for side, lo in ((0, 0), (1, top)):
        @pl.when(jnp.logical_not(has[0][side]))
        def _(lo=lo):
            zero(xe, lo, HALO)
    for side in range(2):
        @pl.when(jnp.logical_not(has[1][side]))
        def _(side=side):
            zero(ry.at[side], 0, top + HALO)

    n = 0
    for i in range(3):
        for side in range(2):
            n = n + has[i][side].astype(jnp.int32)
    pl.semaphore_wait(barrier, n)

    def remote(src, dst, k, i, side):
        return pltpu.make_async_remote_copy(
            src_ref=src, dst_ref=dst, send_sem=send_sem.at[k], recv_sem=recv_sem.at[k],
            device_id=peer(i, side), device_id_type=pl.DeviceIdType.MESH,
        )

    def x_copy(side):
        src = xe.at[:, pl.ds(HALO if side == 0 else size_x, HALO)]
        dst = xe.at[:, pl.ds(top if side == 0 else 0, HALO)]
        return remote(src, dst, side, 0, side)

    def y_copy(side, part):
        lo, count = ((0, HALO), (HALO, size_x), (top, HALO))[part]
        return remote(
            sy.at[side, :, pl.ds(lo, count)], ry.at[1 - side, :, pl.ds(lo, count)],
            2 + 3 * side + part, 1, side,
        )

    def z_copy(side):
        return remote(az.at[side], rz.at[1 - side], 8 + side, 2, side)

    def each(i, action):
        for side in range(2):
            @pl.when(has[i][side])
            def _(side=side):
                action(side)

    each(0, lambda side: x_copy(side).start())
    each(1, lambda side: y_copy(side, 1).start())
    each(0, lambda side: x_copy(1 - side).wait_recv())
    lax.fori_loop(0, HALO, pack_y, 0)
    lax.fori_loop(top, top + HALO, pack_y, 0)
    each(1, lambda side: (y_copy(side, 0).start(), y_copy(side, 2).start()))

    wide = lax.broadcasted_iota(jnp.int32, (2 * HALO + size_y, size_z), 1)

    def fill(x, _):
        for p in range(NARR // 2):
            lo, hi = ry[0, p, x], ry[1, p, x]
            for q in range(2):
                a = 2 * p + q
                own = pltpu.roll(xe[a, x], HALO, 0)
                lo_part = lo if q == 0 else pltpu.roll(lo, HALO, 0)
                hi_part = hi if q == 1 else pltpu.roll(hi, HALO, 0)
                ext[a, x, 0:size_y] = jnp.where(sub < HALO, lo_part, own)
                ext[a, x, size_y : 2 * size_y] = jnp.where(sub < HALO, own, hi_part)
        return 0

    each(1, lambda side: y_copy(1 - side, 1).wait_recv())
    lax.fori_loop(HALO, top, fill, 0)
    each(1, lambda side: (y_copy(1 - side, 0).wait_recv(), y_copy(1 - side, 2).wait_recv()))
    lax.fori_loop(0, HALO, fill, 0)
    lax.fori_loop(top, top + HALO, fill, 0)

    planes = top + HALO

    def pack_z(a, _):
        low = jnp.zeros(wide.shape, jnp.float32)
        high = low
        for x in range(planes):
            spot = (wide >= x * SLOT) & (wide < (x + 1) * SLOT)
            plane = ext[a, x]
            low = jnp.where(spot, pltpu.roll(plane, (x * SLOT + HALO) % size_z, 1), low)
            high = jnp.where(spot, pltpu.roll(plane, (x * SLOT + HALO) % size_z, 1), high)
        az[0, a] = low
        az[1, a] = high
        return 0

    lax.fori_loop(0, NARR, pack_z, 0)
    each(2, lambda side: z_copy(side).start())
    for side in range(2):
        @pl.when(jnp.logical_not(has[2][side]))
        def _(side=side):
            for a in range(NARR):
                rz[side, a] = jnp.zeros(wide.shape, jnp.float32)
    each(2, lambda side: z_copy(1 - side).wait_recv())

    early = lax.rem(wide, SLOT) < HALO
    for a in range(NARR):
        strip[0, a] = jnp.where(early, rz[0, a], az[0, a])
        strip[1, a] = jnp.where(early, az[1, a], rz[1, a])

    rows = 2 * HALO + size_y
    up = lambda v: pltpu.roll(v, rows - 1, 0)
    down = lambda v: pltpu.roll(v, 1, 0)
    zup = lambda v: pltpu.roll(v, size_z - 1, 1)
    zdown = lambda v: pltpu.roll(v, 1, 1)
    xup = lambda v: pltpu.roll(v, size_z - SLOT, 1)
    xdown = lambda v: pltpu.roll(v, SLOT, 1)

    def speed(total):
        return relax / (1.0 + 0.75 * total)

    for s in range(2):
        w = strip[s, 6]
        w = w + xdown(w)
        w = w + down(w)
        if s == 0:
            hz[0] = w
        srate[s] = speed(w + zdown(w))
        for c in range(3):
            sprev[s, c] = strip[s, c]

    first_lane = wide == 0
    last_lane = wide == size_z - 1

    def from_low(v, x):
        return pltpu.roll(v, size_z - HALO + 1 - SLOT * x, 1)

    def from_high(v, x):
        return pltpu.roll(v, size_z - 1 - HALO - SLOT * x, 1)

    def store_terms(x, c, u):
        uz = jnp.where(last_lane, from_high(strip[1, c], x), zup(u))
        for k, term in enumerate(node_terms(u * 0.25, uz * 0.25, up)):
            terms[x, 3 * c + k] = term

    def setup(x, _):
        for c in range(3):
            u = ext[c, x]
            prev[c, x] = u
            store_terms(x, c, u)
        return 0

    def setup_rate(x, _):
        w = ext[6, x - 1] + ext[6, x]
        w = w + down(w)
        rate[x] = speed(w + jnp.where(first_lane, from_low(hz[0], x), zdown(w)))
        return 0

    lax.fori_loop(0, planes, setup, 0)
    lax.fori_loop(1, planes - 1, setup_rate, 0)

    omega = None
    for step in range(ITERS):
        if step == 1:
            omega = 2.0 / (2.0 - radius * radius)
        elif step > 1:
            omega = 4.0 / (4.0 - radius * radius * omega)
        last = step == ITERS - 1

        def strips(s, _):
            low, high = [], []
            for c in range(3):
                u = strip[s, c] * 0.25
                t = node_terms(u, zup(u), up)
                low.append(t)
                high.append([xup(v) for v in t])
            p = stress(stretch(low, high), strip[s, 6])
            for c in range(3):
                mine = p[3 * c : 3 * c + 3]
                minus, plus = node_sums([xdown(v) for v in mine], mine, down)
                hz[3 * s + c] = plus
                u = strip[s, c]
                fresh = advance(
                    u, sprev[s, c], strip[s, 3 + c], strip[s, 7], srate[s],
                    minus + zdown(plus), omega,
                )
                sprev[s, c] = u
                strip[s, c] = fresh
            return 0

        def voxels(x, _):
            low = [[terms[x, 3 * c + k] for k in range(3)] for c in range(3)]
            high = [[terms[x + 1, 3 * c + k] for k in range(3)] for c in range(3)]
            p = stress(stretch(low, high), ext[6, x])
            for k in range(9):
                press[x, k] = p[k]
            return 0

        def nodes(x, _):
            for c in range(3):
                minus, plus = node_sums(
                    [press[x - 1, 3 * c + k] for k in range(3)],
                    [press[x, 3 * c + k] for k in range(3)],
                    down,
                )
                f = minus + jnp.where(first_lane, from_low(hz[c], x), zdown(plus))
                u = ext[c, x]
                fresh = advance(u, prev[c, x], ext[3 + c, x], ext[7, x], rate[x], f, omega)
                if last:
                    out[c, x - HALO] = fresh[HALO : HALO + size_y]
                else:
                    prev[c, x] = u
                    ext[c, x] = fresh
                    store_terms(x, c, fresh)
            return 0

        lax.fori_loop(0, 2, strips, 0)
        lax.fori_loop(step, planes - 1 - step, voxels, 0)
        lax.fori_loop(step + 1, planes - 1 - step, nodes, 0)

    each(0, lambda side: x_copy(side).wait_send())
    each(1, lambda side: [y_copy(side, part).wait_send() for part in range(3)])
    each(2, lambda side: z_copy(side).wait_send())


def per_device(counts, start_disp, inertial, material, pinned, stiffness):
    size_x, size_y, size_z = material.shape
    planes, rows = size_x + 2 * HALO, size_y + 2 * HALO
    assert planes * SLOT == size_z and size_y == 2 * HALO
    vmem = pl.BlockSpec(memory_space=pltpu.VMEM)
    f32 = lambda *shape: pltpu.VMEM(shape, jnp.float32)
    return pl.pallas_call(
        functools.partial(kernel, counts),
        out_shape=jax.ShapeDtypeStruct(start_disp.shape, jnp.float32),
        in_specs=[vmem, vmem, vmem, vmem, pl.BlockSpec(memory_space=pltpu.SMEM)],
        out_specs=vmem,
        scratch_shapes=[
            f32(NARR, planes, size_y, size_z),
            f32(2, NARR // 2, planes, size_y, size_z),
            f32(2, NARR // 2, planes, size_y, size_z),
            f32(NARR, planes, rows, size_z),
            f32(2, NARR, rows, size_z),
            f32(2, NARR, rows, size_z),
            f32(3, planes, rows, size_z),
            f32(planes, rows, size_z),
            f32(planes, 9, rows, size_z),
            f32(planes, 9, rows, size_z),
            f32(2, NARR, rows, size_z),
            f32(2, 3, rows, size_z),
            f32(2, rows, size_z),
            f32(6, rows, size_z),
            pltpu.SemaphoreType.DMA((10,)),
            pltpu.SemaphoreType.DMA((10,)),
        ],
        compiler_params=pltpu.CompilerParams(collective_id=0, has_side_effects=True),
    )(start_disp, inertial, material, pinned, stiffness)


def solution(mesh):
    placed = (
        P(None, "gx", "gy", "gz"),
        P(None, "gx", "gy", "gz"),
        P("gx", "gy", "gz"),
        P("gx", "gy", "gz"),
        P(),
    )
    counts = tuple(mesh.shape[a] for a in AXES)
    return jax.shard_map(
        functools.partial(per_device, counts), mesh=mesh, in_specs=placed,
        out_specs=P(None, "gx", "gy", "gz"), check_vma=False,
    )
```

time: 148 us -> 40.8 us (0.28)
  starting transfers between devices: 58.3 us -> 0 us
  waiting for transfers between devices: 50.8 us -> 0 us
  Pallas kernels: 0 us -> 39.1 us
  other arithmetic: 32.5 us -> 0 us
  local copies, waits for them, and re-layouts: 4.11 us -> 1.54 us
  between operations: 1.78 us -> 0.01 us
    ppermute x24 -> x0, starting transfers between devices: 58.3 us -> none  [the longest x12 39.6 us: with_halo(): lax.ppermute(tail, axis, [(i, (i + 1) % count) for i in range(ends)])]
    ppermute x24 -> x0, waiting for transfers between devices: 50.8 us -> none  [the longest x12 43.1 us: with_halo(): lax.ppermute(head, axis, [((i + 1) % count, i) for i in range(ends)])]
    pallas_call x0 -> x1, Pallas kernels: none -> 39.1 us  [per_device(): pl.pallas_call(functools.partial(kernel, counts), out_shape=jax.ShapeDtyp...]
    sub x52 -> x0, other arithmetic: 11.8 us -> none  [the longest x24 10.1 us: project(): (1.5 if i == j else 0.0) - 0.5 * sum((rotate[k][i] * rotate[k][j] for k i...]
    mul x24 -> x0, other arithmetic: 5.75 us -> none  [project(): welem * (deform[c][d] - rotate[c][d])]
    broadcast_in_dim x1 -> x0, other arithmetic: 4.89 us -> none  [node_halo(): joined = jnp.concatenate([disp, weights[None]], axis=0)]
    concatenate x20 -> x0, other arithmetic: 3.93 us -> none  [the longest x16 3.9 us: with_halo(): jnp.concatenate([lax.ppermute(tail, axis, [(i, (i + 1) % count) for i in...]
    add x120 -> x0, other arithmetic: 3.42 us -> none  [the longest x116 3.11 us: pair_sum(): lax.slice_in_dim(field, 1, size, axis=axis)]
  transfers between devices with their start and end apart: 24 -> 0, of which waited for: 16 -> 0; matrix products, arithmetic and copies ran while one was open for 0% -> 0% of each run, Pallas kernels for 0% -> 0%
where the time goes in v1:
time: 40.8 us; the launch traced here: 40.6 us
  Pallas kernels  39.1 us (96%)
  local copies, waits for them, and re-layouts  1.54 us (4%)
    pallas_call x1, Pallas kernels, per_device(): pl.pallas_call(functools.partial(kernel, counts), out_shape=jax.ShapeDtyp...  39.1 us
    unnamed x1, local copies, waits for them, and re-layouts  1.54 us

profile of v1, /device:TPU:1, one launch (start us, length us, event | category | flops | bytes accessed | tf_op | source)
XLA Modules:
  0.0 40.6 jit_solution(10400231022537199169)
XLA Ops:
  0.0 39.1 %shard_map.55 = f32[3,8,8,128]{3,2,1,0:T(8,128)} custom-call(f32[3,8,8,128]{3,2,1,0:T(8,128)} %start.1, f32[3,8,8,128]{3,2,1,0:T(8,128)} %inertial.1, s32[8,8,128]{2,1,0:T(8,128)} %material.1, s32[8,8,128]{2,1,0:T(8,128)} %pinned.1, f32[8]{0:T(128)} %stiff.1), custom_call_target="tpu_custom_call" | custom-call | tf_op jit(solution)/shard_map/pallas_call | solution.py:365
  39.1 1.5 %copy.7 = f32[3,8,8,128]{3,2,1,0:T(8,128)} copy(f32[3,8,8,128]{3,2,1,0:T(8,128)} %shard_map.55) | data formatting | bytes 196608

commit v2 on v1

--- a/solution.py
+++ b/solution.py
@@ -16,7 +16,19 @@
 HALO = ITERS
 SLOT = 2 * HALO
 NARR = 8
+GROUPS = 2
+PAIRS = NARR // 2 // GROUPS
 AXES = ("gx", "gy", "gz")
+
+
+def loop(lo, hi, body, unroll=2):
+    assert (hi - lo) % unroll == 0
+
+    def group(k, _):
+        body([lo + k * unroll + i for i in range(unroll)])
+        return 0
+
+    lax.fori_loop(0, (hi - lo) // unroll, group, 0)
 
 
 def node_terms(u, uz, roll_y):
@@ -109,32 +121,42 @@
                     barrier, inc=1, device_id=peer(i, side), device_id_type=pl.DeviceIdType.MESH
                 )
 
-    def pack_y(x, _):
-        for p in range(NARR // 2):
-            first, second = xe[2 * p, x], xe[2 * p + 1, x]
-            low = jnp.where(sub < HALO, first, pltpu.roll(second, HALO, 0))
-            high = jnp.where(sub < HALO, pltpu.roll(first, HALO, 0), second)
+    def faces(first, second):
+        low = jnp.where(sub < HALO, first, pltpu.roll(second, HALO, 0))
+        high = jnp.where(sub < HALO, pltpu.roll(first, HALO, 0), second)
+        return low, high
+
+    def pack_y(group, xs):
+        done = [
+            (p, x, faces(xe[2 * p, x], xe[2 * p + 1, x]))
+            for x in xs for p in range(group * PAIRS, (group + 1) * PAIRS)
+        ]
+        for p, x, (low, high) in done:
             sy[0, p, x] = low
             sy[1, p, x] = high
-        return 0
-
-    def own_plane(x, _):
-        mat = material[x]
-        w = jnp.zeros((size_y, size_z), jnp.float32)
-        for index in range(MATS):
-            w = jnp.where(mat == index, quarter[index], w)
-        keep = inside & ((x < size_x - 1) | has[0][1])
-        xe[6, x + HALO] = jnp.where(keep, w, 0.0)
-        pins = pinned[x] > 0
-        xe[7, x + HALO] = jnp.where(pins, 1.0, 0.0)
-        for c in range(3):
-            inert = inertial[c, x]
-            xe[3 + c, x + HALO] = inert
-            xe[c, x + HALO] = jnp.where(pins, inert, start[c, x])
-        pack_y(x + HALO, 0)
-        return 0
-
-    lax.fori_loop(0, size_x, own_plane, 0)
+
+    def own_planes(xs):
+        done = []
+        for x in xs:
+            mat = material[x]
+            w = jnp.zeros((size_y, size_z), jnp.float32)
+            for index in range(MATS):
+                w = jnp.where(mat == index, quarter[index], w)
+            keep = inside & ((x < size_x - 1) | has[0][1])
+            pins = pinned[x] > 0
+            inert = [inertial[c, x] for c in range(3)]
+            arrays = [jnp.where(pins, inert[c], start[c, x]) for c in range(3)] + inert
+            arrays += [jnp.where(keep, w, 0.0), jnp.where(pins, 1.0, 0.0)]
+            done.append((x + HALO, arrays))
+        for x, arrays in done:
+            for a in range(NARR):
+                xe[a, x] = arrays[a]
+            for p in range(NARR // 2):
+                low, high = faces(arrays[2 * p], arrays[2 * p + 1])
+                sy[0, p, x] = low
+                sy[1, p, x] = high
+
+    loop(0, size_x, own_planes)
 
     def zero(ref, lo, n):
         def body(x, _):
@@ -165,20 +187,22 @@
             device_id=peer(i, side), device_id_type=pl.DeviceIdType.MESH,
         )
 
-    def x_copy(side):
-        src = xe.at[:, pl.ds(HALO if side == 0 else size_x, HALO)]
-        dst = xe.at[:, pl.ds(top if side == 0 else 0, HALO)]
-        return remote(src, dst, side, 0, side)
-
-    def y_copy(side, part):
+    def x_copy(side, group):
+        span = pl.ds(2 * PAIRS * group, 2 * PAIRS)
+        src = xe.at[span, pl.ds(HALO if side == 0 else size_x, HALO)]
+        dst = xe.at[span, pl.ds(top if side == 0 else 0, HALO)]
+        return remote(src, dst, 2 * group + side, 0, side)
+
+    def y_copy(side, part, group):
         lo, count = ((0, HALO), (HALO, size_x), (top, HALO))[part]
+        span = pl.ds(PAIRS * group, PAIRS)
         return remote(
-            sy.at[side, :, pl.ds(lo, count)], ry.at[1 - side, :, pl.ds(lo, count)],
-            2 + 3 * side + part, 1, side,
+            sy.at[side, span, pl.ds(lo, count)], ry.at[1 - side, span, pl.ds(lo, count)],
+            2 * GROUPS + (2 * part + side) * GROUPS + group, 1, side,
         )
 
     def z_copy(side):
-        return remote(az.at[side], rz.at[1 - side], 8 + side, 2, side)
+        return remote(az, rz.at[1 - side], 8 * GROUPS + side, 2, side)
 
     def each(i, action):
         for side in range(2):
@@ -186,45 +210,55 @@
             def _(side=side):
                 action(side)
 
-    each(0, lambda side: x_copy(side).start())
-    each(1, lambda side: y_copy(side, 1).start())
-    each(0, lambda side: x_copy(1 - side).wait_recv())
-    lax.fori_loop(0, HALO, pack_y, 0)
-    lax.fori_loop(top, top + HALO, pack_y, 0)
-    each(1, lambda side: (y_copy(side, 0).start(), y_copy(side, 2).start()))
+    for group in range(GROUPS):
+        each(0, lambda side: x_copy(side, group).start())
+        each(1, lambda side: y_copy(side, 1, group).start())
+    for group in range(GROUPS):
+        each(0, lambda side: x_copy(1 - side, group).wait_recv())
+        loop(0, HALO, functools.partial(pack_y, group))
+        loop(top, top + HALO, functools.partial(pack_y, group))
+        for part in (0, 2):
+            each(1, lambda side: y_copy(side, part, group).start())
 
     wide = lax.broadcasted_iota(jnp.int32, (2 * HALO + size_y, size_z), 1)
 
-    def fill(x, _):
-        for p in range(NARR // 2):
-            lo, hi = ry[0, p, x], ry[1, p, x]
-            for q in range(2):
-                a = 2 * p + q
-                own = pltpu.roll(xe[a, x], HALO, 0)
-                lo_part = lo if q == 0 else pltpu.roll(lo, HALO, 0)
-                hi_part = hi if q == 1 else pltpu.roll(hi, HALO, 0)
-                ext[a, x, 0:size_y] = jnp.where(sub < HALO, lo_part, own)
-                ext[a, x, size_y : 2 * size_y] = jnp.where(sub < HALO, own, hi_part)
-        return 0
-
-    each(1, lambda side: y_copy(1 - side, 1).wait_recv())
-    lax.fori_loop(HALO, top, fill, 0)
-    each(1, lambda side: (y_copy(1 - side, 0).wait_recv(), y_copy(1 - side, 2).wait_recv()))
-    lax.fori_loop(0, HALO, fill, 0)
-    lax.fori_loop(top, top + HALO, fill, 0)
+    def fill(xs):
+        done = []
+        for x in xs:
+            for p in range(NARR // 2):
+                lo, hi = ry[0, p, x], ry[1, p, x]
+                for q in range(2):
+                    a = 2 * p + q
+                    own = pltpu.roll(xe[a, x], HALO, 0)
+                    lo_part = lo if q == 0 else pltpu.roll(lo, HALO, 0)
+                    hi_part = hi if q == 1 else pltpu.roll(hi, HALO, 0)
+                    done.append((
+                        a, x, jnp.where(sub < HALO, lo_part, own),
+                        jnp.where(sub < HALO, own, hi_part),
+                    ))
+        for a, x, low, high in done:
+            ext[a, x, 0:size_y] = low
+            ext[a, x, size_y : 2 * size_y] = high
+
+    def arrived(part):
+        for group in range(GROUPS):
+            each(1, lambda side: y_copy(1 - side, part, group).wait_recv())
+
+    arrived(1)
+    loop(HALO, top, fill)
+    arrived(0)
+    arrived(2)
+    loop(0, HALO, fill)
+    loop(top, top + HALO, fill)
 
     planes = top + HALO
 
     def pack_z(a, _):
-        low = jnp.zeros(wide.shape, jnp.float32)
-        high = low
+        packed = jnp.zeros(wide.shape, jnp.float32)
         for x in range(planes):
             spot = (wide >= x * SLOT) & (wide < (x + 1) * SLOT)
-            plane = ext[a, x]
-            low = jnp.where(spot, pltpu.roll(plane, (x * SLOT + HALO) % size_z, 1), low)
-            high = jnp.where(spot, pltpu.roll(plane, (x * SLOT + HALO) % size_z, 1), high)
-        az[0, a] = low
-        az[1, a] = high
+            packed = jnp.where(spot, pltpu.roll(ext[a, x], (x * SLOT + HALO) % size_z, 1), packed)
+        az[a] = packed
         return 0
 
     lax.fori_loop(0, NARR, pack_z, 0)
@@ -238,8 +272,8 @@
 
     early = lax.rem(wide, SLOT) < HALO
     for a in range(NARR):
-        strip[0, a] = jnp.where(early, rz[0, a], az[0, a])
-        strip[1, a] = jnp.where(early, az[1, a], rz[1, a])
+        strip[0, a] = jnp.where(early, rz[0, a], az[a])
+        strip[1, a] = jnp.where(early, az[a], rz[1, a])
 
     rows = 2 * HALO + size_y
     up = lambda v: pltpu.roll(v, rows - 1, 0)
@@ -271,26 +305,33 @@
     def from_high(v, x):
         return pltpu.roll(v, size_z - 1 - HALO - SLOT * x, 1)
 
-    def store_terms(x, c, u):
+    def make_terms(x, c, u):
         uz = jnp.where(last_lane, from_high(strip[1, c], x), zup(u))
-        for k, term in enumerate(node_terms(u * 0.25, uz * 0.25, up)):
-            terms[x, 3 * c + k] = term
-
-    def setup(x, _):
-        for c in range(3):
-            u = ext[c, x]
+        return node_terms(u * 0.25, uz * 0.25, up)
+
+    def put_terms(done):
+        for x, c, three in done:
+            for k in range(3):
+                terms[x, 3 * c + k] = three[k]
+
+    def setup(xs):
+        us = [(x, c, ext[c, x]) for x in xs for c in range(3)]
+        done = [(x, c, make_terms(x, c, u)) for x, c, u in us]
+        for x, c, u in us:
             prev[c, x] = u
-            store_terms(x, c, u)
-        return 0
-
-    def setup_rate(x, _):
-        w = ext[6, x - 1] + ext[6, x]
-        w = w + down(w)
-        rate[x] = speed(w + jnp.where(first_lane, from_low(hz[0], x), zdown(w)))
-        return 0
-
-    lax.fori_loop(0, planes, setup, 0)
-    lax.fori_loop(1, planes - 1, setup_rate, 0)
+        put_terms(done)
+
+    def setup_rate(xs):
+        done = []
+        for x in xs:
+            w = ext[6, x - 1] + ext[6, x]
+            w = w + down(w)
+            done.append(speed(w + jnp.where(first_lane, from_low(hz[0], x), zdown(w))))
+        for x, r in zip(xs, done):
+            rate[x] = r
+
+    loop(0, planes, setup)
+    loop(1, planes - 1, setup_rate)
 
     omega = None
     for step in range(ITERS):
@@ -329,30 +370,37 @@
                 press[x, k] = p[k]
             return 0
 
-        def nodes(x, _):
-            for c in range(3):
-                minus, plus = node_sums(
-                    [press[x - 1, 3 * c + k] for k in range(3)],
-                    [press[x, 3 * c + k] for k in range(3)],
-                    down,
-                )
-                f = minus + jnp.where(first_lane, from_low(hz[c], x), zdown(plus))
-                u = ext[c, x]
-                fresh = advance(u, prev[c, x], ext[3 + c, x], ext[7, x], rate[x], f, omega)
-                if last:
+        def nodes(xs):
+            done = []
+            for x in xs:
+                for c in range(3):
+                    minus, plus = node_sums(
+                        [press[x - 1, 3 * c + k] for k in range(3)],
+                        [press[x, 3 * c + k] for k in range(3)],
+                        down,
+                    )
+                    f = minus + jnp.where(first_lane, from_low(hz[c], x), zdown(plus))
+                    u = ext[c, x]
+                    fresh = advance(u, prev[c, x], ext[3 + c, x], ext[7, x], rate[x], f, omega)
+                    done.append((x, c, u, fresh))
+            if last:
+                for x, c, _, fresh in done:
                     out[c, x - HALO] = fresh[HALO : HALO + size_y]
-                else:
-                    prev[c, x] = u
-                    ext[c, x] = fresh
-                    store_terms(x, c, fresh)
-            return 0
+                return
+            later = [(x, c, make_terms(x, c, fresh)) for x, c, _, fresh in done]
+            for x, c, u, fresh in done:
+                prev[c, x] = u
+                ext[c, x] = fresh
+            put_terms(later)
 
         lax.fori_loop(0, 2, strips, 0)
         lax.fori_loop(step, planes - 1 - step, voxels, 0)
-        lax.fori_loop(step + 1, planes - 1 - step, nodes, 0)
-
-    each(0, lambda side: x_copy(side).wait_send())
-    each(1, lambda side: [y_copy(side, part).wait_send() for part in range(3)])
+        loop(step + 1, planes - 1 - step, nodes)
+
+    for group in range(GROUPS):
+        each(0, lambda side: x_copy(side, group).wait_send())
+        for part in range(3):
+            each(1, lambda side: y_copy(side, part, group).wait_send())
     each(2, lambda side: z_copy(side).wait_send())
 
 
@@ -372,7 +420,7 @@
             f32(2, NARR // 2, planes, size_y, size_z),
             f32(2, NARR // 2, planes, size_y, size_z),
             f32(NARR, planes, rows, size_z),
-            f32(2, NARR, rows, size_z),
+            f32(NARR, rows, size_z),
             f32(2, NARR, rows, size_z),
             f32(3, planes, rows, size_z),
             f32(planes, rows, size_z),
@@ -382,8 +430,8 @@
             f32(2, 3, rows, size_z),
             f32(2, rows, size_z),
             f32(6, rows, size_z),
-            pltpu.SemaphoreType.DMA((10,)),
-            pltpu.SemaphoreType.DMA((10,)),
+            pltpu.SemaphoreType.DMA((8 * GROUPS + 2,)),
+            pltpu.SemaphoreType.DMA((8 * GROUPS + 2,)),
         ],
         compiler_params=pltpu.CompilerParams(collective_id=0, has_side_effects=True),
     )(start_disp, inertial, material, pinned, stiffness)

time: 40.8 us -> 35.8 us (0.88)
  Pallas kernels: 39.1 us -> 34 us
    pallas_call x1, Pallas kernels: 39.1 us -> 34 us  [per_device(): pl.pallas_call(functools.partial(kernel, counts), out_shape=jax.ShapeDtyp...]
where the time goes in v2:
time: 35.8 us; the launch traced here: 35.6 us
  Pallas kernels  34 us (95%)
  local copies, waits for them, and re-layouts  1.54 us (4%)
    pallas_call x1, Pallas kernels, per_device(): pl.pallas_call(functools.partial(kernel, counts), out_shape=jax.ShapeDtyp...  34 us
    unnamed x1, local copies, waits for them, and re-layouts  1.54 us

profile of v2, /device:TPU:1, one launch (start us, length us, event | category | flops | bytes accessed | tf_op | source)
XLA Modules:
  0.0 35.6 jit_solution(9766067844192563610)
XLA Ops:
  0.0 34.0 %shard_map.55 = f32[3,8,8,128]{3,2,1,0:T(8,128)} custom-call(f32[3,8,8,128]{3,2,1,0:T(8,128)} %start.1, f32[3,8,8,128]{3,2,1,0:T(8,128)} %inertial.1, s32[8,8,128]{2,1,0:T(8,128)} %material.1, s32[8,8,128]{2,1,0:T(8,128)} %pinned.1, f32[8]{0:T(128)} %stiff.1), custom_call_target="tpu_custom_call" | custom-call | tf_op jit(solution)/shard_map/pallas_call | solution.py:413
  34.1 1.5 %copy.7 = f32[3,8,8,128]{3,2,1,0:T(8,128)} copy(f32[3,8,8,128]{3,2,1,0:T(8,128)} %shard_map.55) | data formatting | bytes 196608

commit v3 on v2

--- a/solution.py
+++ b/solution.py
@@ -170,6 +170,8 @@
         @pl.when(jnp.logical_not(has[0][side]))
         def _(lo=lo):
             zero(xe, lo, HALO)
+            for row in range(2):
+                zero(ry.at[row, pl.ds(PAIRS, PAIRS)], lo, HALO)
     for side in range(2):
         @pl.when(jnp.logical_not(has[1][side]))
         def _(side=side):
@@ -201,6 +203,14 @@
             2 * GROUPS + (2 * part + side) * GROUPS + group, 1, side,
         )
 
+    def corner(row, side):
+        span = pl.ds(PAIRS, PAIRS)
+        return remote(
+            ry.at[row, span, pl.ds(HALO if side == 0 else size_x, HALO)],
+            ry.at[row, span, pl.ds(top if side == 0 else 0, HALO)],
+            8 * GROUPS + 2 + 2 * row + side, 0, side,
+        )
+
     def z_copy(side):
         return remote(az, rz.at[1 - side], 8 * GROUPS + side, 2, side)
 
@@ -213,12 +223,13 @@
     for group in range(GROUPS):
         each(0, lambda side: x_copy(side, group).start())
         each(1, lambda side: y_copy(side, 1, group).start())
-    for group in range(GROUPS):
-        each(0, lambda side: x_copy(1 - side, group).wait_recv())
-        loop(0, HALO, functools.partial(pack_y, group))
-        loop(top, top + HALO, functools.partial(pack_y, group))
-        for part in (0, 2):
-            each(1, lambda side: y_copy(side, part, group).start())
+    each(0, lambda side: x_copy(1 - side, 0).wait_recv())
+    loop(0, HALO, functools.partial(pack_y, 0))
+    loop(top, top + HALO, functools.partial(pack_y, 0))
+    for part in (0, 2):
+        each(1, lambda side: y_copy(side, part, 0).start())
+    each(1, lambda row: y_copy(1 - row, 1, 1).wait_recv())
+    each(1, lambda row: each(0, lambda side: corner(row, side).start()))
 
     wide = lax.broadcasted_iota(jnp.int32, (2 * HALO + size_y, size_z), 1)
 
@@ -240,14 +251,12 @@
             ext[a, x, 0:size_y] = low
             ext[a, x, size_y : 2 * size_y] = high
 
-    def arrived(part):
-        for group in range(GROUPS):
-            each(1, lambda side: y_copy(1 - side, part, group).wait_recv())
-
-    arrived(1)
+    each(1, lambda row: y_copy(1 - row, 1, 0).wait_recv())
     loop(HALO, top, fill)
-    arrived(0)
-    arrived(2)
+    each(0, lambda side: x_copy(1 - side, 1).wait_recv())
+    for part in (0, 2):
+        each(1, lambda row: y_copy(1 - row, part, 0).wait_recv())
+    each(1, lambda row: each(0, lambda side: corner(row, 1 - side).wait_recv()))
     loop(0, HALO, fill)
     loop(top, top + HALO, fill)
 
@@ -341,26 +350,31 @@
             omega = 4.0 / (4.0 - radius * radius * omega)
         last = step == ITERS - 1
 
-        def strips(s, _):
-            low, high = [], []
-            for c in range(3):
-                u = strip[s, c] * 0.25
-                t = node_terms(u, zup(u), up)
-                low.append(t)
-                high.append([xup(v) for v in t])
-            p = stress(stretch(low, high), strip[s, 6])
-            for c in range(3):
-                mine = p[3 * c : 3 * c + 3]
-                minus, plus = node_sums([xdown(v) for v in mine], mine, down)
-                hz[3 * s + c] = plus
-                u = strip[s, c]
-                fresh = advance(
-                    u, sprev[s, c], strip[s, 3 + c], strip[s, 7], srate[s],
-                    minus + zdown(plus), omega,
-                )
-                sprev[s, c] = u
-                strip[s, c] = fresh
-            return 0
+        def strips():
+            done = []
+            for s in range(2):
+                low, high = [], []
+                for c in range(3):
+                    u = strip[s, c] * 0.25
+                    t = node_terms(u, zup(u), up)
+                    low.append(t)
+                    high.append([xup(v) for v in t])
+                p = stress(stretch(low, high), strip[s, 6])
+                for c in range(3):
+                    mine = p[3 * c : 3 * c + 3]
+                    minus, plus = node_sums([xdown(v) for v in mine], mine, down)
+                    u = strip[s, c]
+                    fresh = advance(
+                        u, sprev[s, c], strip[s, 3 + c], strip[s, 7], srate[s],
+                        minus + zdown(plus), omega,
+                    )
+                    done.append((s, c, u, plus, fresh))
+            for s, c, u, plus, fresh in done:
+                if s == 0:
+                    hz[c] = plus
+                if not last:
+                    sprev[s, c] = u
+                    strip[s, c] = fresh
 
         def voxels(x, _):
             low = [[terms[x, 3 * c + k] for k in range(3)] for c in range(3)]
@@ -393,14 +407,16 @@
                 ext[c, x] = fresh
             put_terms(later)
 
-        lax.fori_loop(0, 2, strips, 0)
+        strips()
         lax.fori_loop(step, planes - 1 - step, voxels, 0)
         loop(step + 1, planes - 1 - step, nodes)
 
     for group in range(GROUPS):
         each(0, lambda side: x_copy(side, group).wait_send())
-        for part in range(3):
-            each(1, lambda side: y_copy(side, part, group).wait_send())
+        each(1, lambda side: y_copy(side, 1, group).wait_send())
+    for part in (0, 2):
+        each(1, lambda side: y_copy(side, part, 0).wait_send())
+    each(1, lambda row: each(0, lambda side: corner(row, side).wait_send()))
     each(2, lambda side: z_copy(side).wait_send())
 
 
@@ -429,9 +445,9 @@
             f32(2, NARR, rows, size_z),
             f32(2, 3, rows, size_z),
             f32(2, rows, size_z),
-            f32(6, rows, size_z),
-            pltpu.SemaphoreType.DMA((8 * GROUPS + 2,)),
-            pltpu.SemaphoreType.DMA((8 * GROUPS + 2,)),
+            f32(3, rows, size_z),
+            pltpu.SemaphoreType.DMA((8 * GROUPS + 6,)),
+            pltpu.SemaphoreType.DMA((8 * GROUPS + 6,)),
         ],
         compiler_params=pltpu.CompilerParams(collective_id=0, has_side_effects=True),
     )(start_disp, inertial, material, pinned, stiffness)

time: 35.8 us -> 33.9 us (0.947)
  Pallas kernels: 34 us -> 32.2 us
    pallas_call x1, Pallas kernels: 34 us -> 32.2 us  [per_device(): pl.pallas_call(functools.partial(kernel, counts), out_shape=jax.ShapeDtyp...]
where the time goes in v3:
time: 33.9 us; the launch traced here: 33.7 us
  Pallas kernels  32.2 us (95%)
  local copies, waits for them, and re-layouts  1.54 us (5%)
    pallas_call x1, Pallas kernels, per_device(): pl.pallas_call(functools.partial(kernel, counts), out_shape=jax.ShapeDtyp...  32.2 us
    unnamed x1, local copies, waits for them, and re-layouts  1.54 us

profile of v3, /device:TPU:1, one launch (start us, length us, event | category | flops | bytes accessed | tf_op | source)
XLA Modules:
  0.0 33.7 jit_solution(7956336063847198326)
XLA Ops:
  0.0 32.2 %shard_map.55 = f32[3,8,8,128]{3,2,1,0:T(8,128)} custom-call(f32[3,8,8,128]{3,2,1,0:T(8,128)} %start.1, f32[3,8,8,128]{3,2,1,0:T(8,128)} %inertial.1, s32[8,8,128]{2,1,0:T(8,128)} %material.1, s32[8,8,128]{2,1,0:T(8,128)} %pinned.1, f32[8]{0:T(128)} %stiff.1), custom_call_target="tpu_custom_call" | custom-call | tf_op jit(solution)/shard_map/pallas_call | solution.py:429
  32.2 1.5 %copy.7 = f32[3,8,8,128]{3,2,1,0:T(8,128)} copy(f32[3,8,8,128]{3,2,1,0:T(8,128)} %shard_map.55) | data formatting | bytes 196608

commit v4 on v3

--- a/solution.py
+++ b/solution.py
@@ -156,7 +156,7 @@
                 sy[0, p, x] = low
                 sy[1, p, x] = high
 
-    loop(0, size_x, own_planes)
+    loop(0, size_x, own_planes, 4)
 
     def zero(ref, lo, n):
         def body(x, _):
@@ -224,8 +224,8 @@
         each(0, lambda side: x_copy(side, group).start())
         each(1, lambda side: y_copy(side, 1, group).start())
     each(0, lambda side: x_copy(1 - side, 0).wait_recv())
-    loop(0, HALO, functools.partial(pack_y, 0))
-    loop(top, top + HALO, functools.partial(pack_y, 0))
+    loop(0, HALO, functools.partial(pack_y, 0), HALO)
+    loop(top, top + HALO, functools.partial(pack_y, 0), HALO)
     for part in (0, 2):
         each(1, lambda side: y_copy(side, part, 0).start())
     each(1, lambda row: y_copy(1 - row, 1, 1).wait_recv())
@@ -252,26 +252,48 @@
             ext[a, x, size_y : 2 * size_y] = high
 
     each(1, lambda row: y_copy(1 - row, 1, 0).wait_recv())
-    loop(HALO, top, fill)
+    loop(HALO, top, fill, 4)
     each(0, lambda side: x_copy(1 - side, 1).wait_recv())
     for part in (0, 2):
         each(1, lambda row: y_copy(1 - row, part, 0).wait_recv())
     each(1, lambda row: each(0, lambda side: corner(row, 1 - side).wait_recv()))
-    loop(0, HALO, fill)
-    loop(top, top + HALO, fill)
+    loop(0, HALO, fill, HALO)
+    loop(top, top + HALO, fill, HALO)
 
     planes = top + HALO
 
-    def pack_z(a, _):
-        packed = jnp.zeros(wide.shape, jnp.float32)
+    def pack_z(arrays):
+        packed = [jnp.zeros(wide.shape, jnp.float32) for _ in arrays]
         for x in range(planes):
             spot = (wide >= x * SLOT) & (wide < (x + 1) * SLOT)
-            packed = jnp.where(spot, pltpu.roll(ext[a, x], (x * SLOT + HALO) % size_z, 1), packed)
-        az[a] = packed
-        return 0
-
-    lax.fori_loop(0, NARR, pack_z, 0)
+            for k, a in enumerate(arrays):
+                moved = pltpu.roll(ext[a, x], (x * SLOT + HALO) % size_z, 1)
+                packed[k] = jnp.where(spot, moved, packed[k])
+        for a, value in zip(arrays, packed):
+            az[a] = value
+
+    loop(0, NARR, pack_z, 4)
     each(2, lambda side: z_copy(side).start())
+
+    rows = 2 * HALO + size_y
+    up = lambda v: pltpu.roll(v, rows - 1, 0)
+    down = lambda v: pltpu.roll(v, 1, 0)
+    zup = lambda v: pltpu.roll(v, size_z - 1, 1)
+    zdown = lambda v: pltpu.roll(v, 1, 1)
+
+    def begin(xs):
+        us = [(x, c, ext[c, x]) for x in xs for c in range(3)]
+        for x, c, u in us:
+            prev[c, x] = u
+
+    def weigh(xs):
+        sums = [ext[6, x - 1] + ext[6, x] for x in xs]
+        sums = [w + down(w) for w in sums]
+        for x, w in zip(xs, sums):
+            rate[x] = w
+
+    loop(0, planes, begin, 4)
+    loop(1, planes - 1, weigh, (planes - 2) // 2)
     for side in range(2):
         @pl.when(jnp.logical_not(has[2][side]))
         def _(side=side):
@@ -284,11 +306,6 @@
         strip[0, a] = jnp.where(early, rz[0, a], az[a])
         strip[1, a] = jnp.where(early, az[a], rz[1, a])
 
-    rows = 2 * HALO + size_y
-    up = lambda v: pltpu.roll(v, rows - 1, 0)
-    down = lambda v: pltpu.roll(v, 1, 0)
-    zup = lambda v: pltpu.roll(v, size_z - 1, 1)
-    zdown = lambda v: pltpu.roll(v, 1, 1)
     xup = lambda v: pltpu.roll(v, size_z - SLOT, 1)
     xdown = lambda v: pltpu.roll(v, SLOT, 1)
 
@@ -326,21 +343,18 @@
     def setup(xs):
         us = [(x, c, ext[c, x]) for x in xs for c in range(3)]
         done = [(x, c, make_terms(x, c, u)) for x, c, u in us]
-        for x, c, u in us:
-            prev[c, x] = u
         put_terms(done)
 
     def setup_rate(xs):
         done = []
         for x in xs:
-            w = ext[6, x - 1] + ext[6, x]
-            w = w + down(w)
+            w = rate[x]
             done.append(speed(w + jnp.where(first_lane, from_low(hz[0], x), zdown(w))))
         for x, r in zip(xs, done):
             rate[x] = r
 
-    loop(0, planes, setup)
-    loop(1, planes - 1, setup_rate)
+    loop(0, planes, setup, 4)
+    loop(1, planes - 1, setup_rate, (planes - 2) // 2)
 
     omega = None
     for step in range(ITERS):

time: 33.9 us -> 32.8 us (0.968)
  Pallas kernels: 32.2 us -> 31.1 us
    pallas_call x1, Pallas kernels: 32.2 us -> 31.1 us  [per_device(): pl.pallas_call(functools.partial(kernel, counts), out_shape=jax.ShapeDtyp...]
where the time goes in v4:
time: 32.8 us; the launch traced here: 32.7 us
  Pallas kernels  31.1 us (95%)
  local copies, waits for them, and re-layouts  1.54 us (5%)
    pallas_call x1, Pallas kernels, per_device(): pl.pallas_call(functools.partial(kernel, counts), out_shape=jax.ShapeDtyp...  31.1 us
    unnamed x1, local copies, waits for them, and re-layouts  1.54 us

profile of v4, /device:TPU:1, one launch (start us, length us, event | category | flops | bytes accessed | tf_op | source)
XLA Modules:
  0.0 32.7 jit_solution(16575325728091253471)
XLA Ops:
  0.0 31.1 %shard_map.55 = f32[3,8,8,128]{3,2,1,0:T(8,128)} custom-call(f32[3,8,8,128]{3,2,1,0:T(8,128)} %start.1, f32[3,8,8,128]{3,2,1,0:T(8,128)} %inertial.1, s32[8,8,128]{2,1,0:T(8,128)} %material.1, s32[8,8,128]{2,1,0:T(8,128)} %pinned.1, f32[8]{0:T(128)} %stiff.1), custom_call_target="tpu_custom_call" | custom-call | tf_op jit(solution)/shard_map/pallas_call | solution.py:443
  31.1 1.5 %copy.7 = f32[3,8,8,128]{3,2,1,0:T(8,128)} copy(f32[3,8,8,128]{3,2,1,0:T(8,128)} %shard_map.55) | data formatting | bytes 196608
